TPU v7x, 32 devices: a whole 2x2x4 slice. The times are simulated.
32 devices in a mesh: dp: 16 (over z, y, core), tp: 2 (over x).
Axes of the slice: x: 2, y: 2, z: 4, core: 2. Of those that a mesh axis runs over, the one named last changes fastest.
Arguments:
- activations: bfloat16 [2048, 2304], P('dp'), may hold values from -6 to 6
- out_grads: bfloat16 [2048, 2048], P('dp', 'tp'), may hold values from -6 to 6
- right_prev: float32 [2048, 128], P('tp'), may hold values from -6 to 6
Outputs:
- update: float32 [2304, 2048], P('dp', 'tp')
- residual: bfloat16 [36864, 2048], P('dp', 'tp')
All inputs are finite; a program needn't handle non-finite values.
Results may differ from a plain program's by a relative error of at most 0.001.
Values sent between devices are 32-bit elements; how exact they have to be, the bound alone decides.
No kernel may reach another device: no remote copies, remote signals or barrier semaphores. Data moves between devices by JAX's collectives and lax.ppermute only.
A program may use at most 64 MiB of HBM per device.

v0:
```python
import jax
import jax.numpy as jnp
from jax import lax
from jax.sharding import PartitionSpec as P


def gram_of(left_rows):
    return jnp.dot(left_rows.T, left_rows, precision=lax.Precision.HIGHEST)


def finish(left_rows, gram_matrix):
    ridge = 1e-06 * jnp.trace(gram_matrix) / gram_matrix.shape[0]
    gram_matrix = gram_matrix + ridge * jnp.eye(gram_matrix.shape[0], dtype=gram_matrix.dtype)
    lower = jnp.linalg.cholesky(gram_matrix)
    return jax.scipy.linalg.solve_triangular(lower, left_rows.T, lower=True).T


def per_device(activations, out_grads, right_prev):
    gradient = jnp.dot(activations.T, out_grads, preferred_element_type=jnp.float32)
    left_part = jnp.dot(gradient, right_prev, precision=lax.Precision.HIGHEST)
    left_sum = lax.psum(left_part, ("dp", "tp"))
    left_basis = finish(left_sum, gram_of(left_sum))
    right_part = jnp.dot(gradient.T, left_basis, precision=lax.Precision.HIGHEST)
    right_factor = lax.psum(right_part, "dp") / lax.axis_size("dp")
    update_full = jnp.dot(left_basis, right_factor.T, precision=lax.Precision.HIGHEST)
    residual = (gradient - update_full).astype(jnp.bfloat16)
    rows_dev = update_full.shape[0] // lax.axis_size("dp")
    first_row = lax.axis_index("dp") * rows_dev
    update = lax.dynamic_slice_in_dim(update_full, first_row, rows_dev, 0)
    return (update, residual)


def solution(mesh):
    in_specs = (P("dp", None), P("dp", "tp"), P("tp", None))
    out_specs = (P("dp", "tp"), P("dp", "tp"))
    return jax.shard_map(
        per_device, mesh=mesh, in_specs=in_specs, out_specs=out_specs, check_vma=False
    )
```

profile of v0, /device:TPU:0, one launch (start us, length us, event | category | flops | bytes accessed | tf_op | source)
XLA Modules:
  0.0 314.1 jit_solution(11109167322946106435)
XLA Ops:
  7.2 0.0 copy-start
  7.2 0.0 copy-start.3
  7.2 0.0 all-reduce.3.cloned.1.call-start
  7.2 1.0 copy-done
  8.2 2.4 fusion.9
  10.6 0.0 copy-start.1
  10.6 3.6 %copy-done.1 = f32[2304,1024]{1,0:T(8,128)} copy-done((f32[2304,1024]{1,0:T(8,128)}, f32[2304,1024]{1,0:T(8,128)S(1)}, u32[]{:S(2)}) %copy-start.1) | copy-done | bytes 9437208
  14.2 0.0 copy-done.3
  14.2 8.6 %fusion.10 = f32[2304,128]{1,0:T(8,128)} fusion(f32[2304,1024]{1,0:T(8,128)S(1)} %fusion.9, f32[1024,128]{1,0:T(8,128)S(1)} %copy-done.3), kind=kOutput, calls=%fused_computation.20 | convolution fusion | flops 3623878656 | bytes 11141120 | tf_op jit(solution)/shard_map/dot_general | solution.py:20
  22.8 0.0 all-reduce.3.cloned.1.call-update
  22.8 0.2 all-reduce.5.cloned.1.call-start
  23.0 134.3 %all-reduce.3.cloned.1.call-done = f32[2304,128]{1,0:T(8,128)} async-done(((f32[2304,128]{1,0:T(8,128)}), f32[2304,128]{1,0:T(8,128)}) %all-reduce.3.cloned.1.call-update) | async-done | bytes 1179664 | tf_op jit(solution)/shard_map/psum | solution.py:21
  157.4 0.0 copy-start.2
  157.4 4.3 %select_reduce_fusion.1 = (f32[]{:T(128)}, f32[128,128]{1,0:T(8,128)S(1)}) fusion(f32[2304,128]{1,0:T(8,128)} %all-reduce.3.cloned.1.call-done), kind=kOutput, calls=%fused_computation.13 | convolution fusion | flops 453033984 | bytes 1245188 | tf_op jit(solution)/shard_map/dot_general | solution.py:8
  161.7 0.1 copy.5
  162.5 11.7 %cholesky.17 = f32[128,128]{1,0:T(8,128)S(1)} custom-call(f32[128,128]{1,0:T(8,128)S(1)} %fusion.7), custom_call_target="Cholesky" | custom-call | tf_op jit(solution)/shard_map/jit(cholesky)/cholesky | solution.py:14
  174.2 0.6 compare_reduce_fusion
  174.9 0.7 fusion.3
  175.5 9.8 %custom-call.7 = f32[1,128,128]{1,2,0:T(8,128)S(1)} custom-call(f32[1,128,128]{2,1,0:T(8,128)S(1)} %fusion.3), custom_call_target="InvertDiagBlocksLowerTriangular" | custom-call | tf_op jit(solution)/shard_map/jit(_solve_triangular)/triangular_solve | solution.py:15
  185.4 0.0 copy-done.2
  185.4 1.2 fusion.4
  186.6 18.2 %fusion.11 = f32[1024,128]{1,0:T(8,128)} fusion(f32[2304,1024]{1,0:T(8,128)} %copy-done.1, f32[128,2304]{1,0:T(8,128)S(1)} %fusion.4), kind=kOutput, calls=%fused_computation.21 | convolution fusion | flops 3623878656 | bytes 11141120 | tf_op jit(solution)/shard_map/dot_general | solution.py:23
  204.8 0.0 all-reduce.5.cloned.1.call-update
  204.8 89.8 %all-reduce.5.cloned.1.call-done = f32[1024,128]{1,0:T(8,128)} async-done(((f32[1024,128]{1,0:T(8,128)}), f32[1024,128]{1,0:T(8,128)}) %all-reduce.5.cloned.1.call-update) | async-done | bytes 524304 | tf_op jit(solution)/shard_map/psum | solution.py:24
  294.6 11.8 %subtract_convert_fusion = (bf16[2304,1024]{1,0:T(8,128)(2,1)}, f32[2304,1024]{1,0:T(8,128)S(1)}) fusion(f32[2304,1024]{1,0:T(8,128)} %copy-done.1, f32[128,2304]{1,0:T(8,128)S(1)} %fusion.4, f32[1024,128]{1,0:T(8,128)} %all-reduce.5.cloned.1.call-done), kind=kOutput, calls=%fused_computation | convolution fusion | flops 3628728320 | bytes 25296896 | tf_op jit(solution)/shard_map/dot_general | solution.py:25
  306.4 0.9 constant_dynamic-slice_fusion
  (2 shorter events, 0.1 us)
Async XLA Ops:
  7.2 1.1 copy-start
  7.2 7.0 %copy-start.3 = (f32[1024,128]{1,0:T(8,128)S(1)}, f32[1024,128]{1,0:T(8,128)}, u32[]{:S(2)}) copy-start(f32[1024,128]{1,0:T(8,128)} %param.5) | copy-start | bytes 1572868
  7.2 150.2 %all-reduce.3.cloned.1.call-start = ((), (), s32[]{:S(2)}) async-start(), calls=%async_computation | async-start | bytes 2359296 | tf_op jit(solution)/shard_map/psum | solution.py:21
  10.6 3.6 %copy-start.1 = (f32[2304,1024]{1,0:T(8,128)}, f32[2304,1024]{1,0:T(8,128)S(1)}, u32[]{:S(2)}) copy-start(f32[2304,1024]{1,0:T(8,128)S(1)} %fusion.9) | copy-start | bytes 28311556
  22.8 271.8 %all-reduce.5.cloned.1.call-start = ((), (), s32[]{:S(2)}) async-start(), calls=%async_computation.1 | async-start | bytes 1048576 | tf_op jit(solution)/shard_map/psum | solution.py:24
  157.4 28.0 %copy-start.2 = (f32[2304,128]{1,0:T(8,128)S(1)}, f32[2304,128]{1,0:T(8,128)}, u32[]{:S(2)}) copy-start(f32[2304,128]{1,0:T(8,128)} %all-reduce.3.cloned.1.call-done) | copy-start | bytes 3538948
Sparse Core Ops, SparseCore 0:
  22.9 134.3 all-reduce.2
  204.9 89.6 all-reduce.4
where the time goes:
time: 314 us
  waiting for transfers between devices  224 us (71%)
  matrix products  46.5 us (15%)
  other arithmetic  22.9 us (7%)
  between operations  14.8 us (5%)
  local copies, waits for them, and re-layouts  5.59 us (2%)
    psum x1, waiting for transfers between devices, per_device(): left_sum = lax.psum(left_part, ('dp', 'tp'))  134 us
    psum x1, waiting for transfers between devices, per_device(): right_factor = lax.psum(right_part, 'dp') / lax.axis_size('dp')  89.8 us
    dot_general x1, matrix products, per_device(): jnp.dot(gradient.T, left_basis, precision=lax.Precision.HIGHEST)  18.2 us
    another operation x3, other arithmetic, finish(): lower = jnp.linalg.cholesky(gram_matrix)  12.4 us
    dot_general x1, matrix products, per_device(): jnp.dot(left_basis, right_factor.T, precision=lax.Precision.HIGHEST)  11.8 us
    another operation x2, other arithmetic, finish(): return jax.scipy.linalg.solve_triangular(lower, left_rows.T, lower=True).T  10.5 us
    dot_general x1, matrix products, per_device(): left_part = jnp.dot(gradient, right_prev, precision=lax.Precision.HIGHEST)  8.57 us
  transfers between devices with their start and end apart: 2, of which 2 were waited for; matrix products, arithmetic and copies ran while one was open for 0% of the time, Pallas kernels for 0%

commit v1 on v0

--- a/solution.py
+++ b/solution.py
@@ -16,12 +16,18 @@
 
 
 def per_device(activations, out_grads, right_prev):
+
+    def streams_begin(buf):
+        row_out = lax.all_gather(buf, axis_name="dp")
+        upper = jnp.sum(row_out, axis=0)
+        return upper
+
     gradient = jnp.dot(activations.T, out_grads, preferred_element_type=jnp.float32)
     left_part = jnp.dot(gradient, right_prev, precision=lax.Precision.HIGHEST)
     left_sum = lax.psum(left_part, ("dp", "tp"))
     left_basis = finish(left_sum, gram_of(left_sum))
     right_part = jnp.dot(gradient.T, left_basis, precision=lax.Precision.HIGHEST)
-    right_factor = lax.psum(right_part, "dp") / lax.axis_size("dp")
+    right_factor = streams_begin(right_part) / lax.axis_size("dp")
     update_full = jnp.dot(left_basis, right_factor.T, precision=lax.Precision.HIGHEST)
     residual = (gradient - update_full).astype(jnp.bfloat16)
     rows_dev = update_full.shape[0] // lax.axis_size("dp")

time: 314 us -> 302 us (0.962)
  waiting for transfers between devices: 224 us -> 208 us
  other arithmetic: 22.9 us -> 26.7 us
    psum x1 -> x0, waiting for transfers between devices: 89.8 us -> none  [per_device(): right_factor = lax.psum(right_part, 'dp') / lax.axis_size('dp')]
    all_gather x0 -> x1, waiting for transfers between devices: none -> 73.4 us  [streams_begin(): row_out = lax.all_gather(buf, axis_name='dp')]
    reduce_sum x0 -> x1, other arithmetic: none -> 3.82 us  [streams_begin(): upper = jnp.sum(row_out, axis=0)]
where the time goes in v1:
time: 302 us; the launch traced here: 301 us
  waiting for transfers between devices  208 us (69%)
  matrix products  46.4 us (15%)
  other arithmetic  26.7 us (9%)
  between operations  14.8 us (5%)
  local copies, waits for them, and re-layouts  5.59 us (2%)
    psum x1, waiting for transfers between devices, per_device(): left_sum = lax.psum(left_part, ('dp', 'tp'))  134 us
    all_gather x1, waiting for transfers between devices, streams_begin(): row_out = lax.all_gather(buf, axis_name='dp')  73.4 us
    dot_general x1, matrix products, per_device(): jnp.dot(gradient.T, left_basis, precision=lax.Precision.HIGHEST)  18.2 us
    another operation x3, other arithmetic, finish(): lower = jnp.linalg.cholesky(gram_matrix)  12.4 us
    dot_general x1, matrix products, per_device(): jnp.dot(left_basis, right_factor.T, precision=lax.Precision.HIGHEST)  11.7 us
    another operation x2, other arithmetic, finish(): return jax.scipy.linalg.solve_triangular(lower, left_rows.T, lower=True).T  10.5 us
    dot_general x1, matrix products, per_device(): left_part = jnp.dot(gradient, right_prev, precision=lax.Precision.HIGHEST)  8.57 us
  transfers between devices with their start and end apart: 2, of which 2 were waited for; matrix products, arithmetic and copies ran while one was open for 0% of the time, Pallas kernels for 0%

profile of v1, /device:TPU:0, one launch (start us, length us, event | category | flops | bytes accessed | tf_op | source)
XLA Modules:
  0.0 301.4 jit_solution(9764014253778824206)
XLA Ops:
  7.2 0.0 copy-start
  7.2 0.0 copy-start.3
  7.2 0.0 all-reduce.2.cloned.1.call-start
  7.2 1.0 copy-done
  8.2 2.4 fusion.9
  10.6 0.0 copy-start.1
  10.6 3.6 %copy-done.1 = f32[2304,1024]{1,0:T(8,128)} copy-done((f32[2304,1024]{1,0:T(8,128)}, f32[2304,1024]{1,0:T(8,128)S(1)}, u32[]{:S(2)}) %copy-start.1) | copy-done | bytes 9437208
  14.2 0.0 copy-done.3
  14.2 8.6 %fusion.10 = f32[2304,128]{1,0:T(8,128)} fusion(f32[2304,1024]{1,0:T(8,128)S(1)} %fusion.9, f32[1024,128]{1,0:T(8,128)S(1)} %copy-done.3), kind=kOutput, calls=%fused_computation.20 | convolution fusion | flops 3623878656 | bytes 11141120 | tf_op jit(solution)/shard_map/dot_general | solution.py:26
  22.8 0.0 all-reduce.2.cloned.1.call-update
  22.8 0.2 all-gather.3.cloned.1.call-start
  23.0 134.3 %all-reduce.2.cloned.1.call-done = f32[2304,128]{1,0:T(8,128)} async-done(((f32[2304,128]{1,0:T(8,128)}), f32[2304,128]{1,0:T(8,128)}) %all-reduce.2.cloned.1.call-update) | async-done | bytes 1179664 | tf_op jit(solution)/shard_map/psum | solution.py:27
  157.4 0.0 copy-start.2
  157.4 4.3 %select_reduce_fusion.1 = (f32[]{:T(128)}, f32[128,128]{1,0:T(8,128)S(1)}) fusion(f32[2304,128]{1,0:T(8,128)} %all-reduce.2.cloned.1.call-done), kind=kOutput, calls=%fused_computation.13 | convolution fusion | flops 453033984 | bytes 1245188 | tf_op jit(solution)/shard_map/dot_general | solution.py:8
  161.7 0.1 copy.5
  162.5 11.7 %cholesky.17 = f32[128,128]{1,0:T(8,128)S(1)} custom-call(f32[128,128]{1,0:T(8,128)S(1)} %fusion.7), custom_call_target="Cholesky" | custom-call | tf_op jit(solution)/shard_map/jit(cholesky)/cholesky | solution.py:14
  174.2 0.6 compare_reduce_fusion
  174.9 0.7 fusion.3
  175.5 9.8 %custom-call.7 = f32[1,128,128]{1,2,0:T(8,128)S(1)} custom-call(f32[1,128,128]{2,1,0:T(8,128)S(1)} %fusion.3), custom_call_target="InvertDiagBlocksLowerTriangular" | custom-call | tf_op jit(solution)/shard_map/jit(_solve_triangular)/triangular_solve | solution.py:15
  185.4 0.0 copy-done.2
  185.4 1.2 fusion.4
  186.6 18.2 %fusion.11 = f32[1024,128]{1,0:T(8,128)} fusion(f32[2304,1024]{1,0:T(8,128)} %copy-done.1, f32[128,2304]{1,0:T(8,128)S(1)} %fusion.4), kind=kOutput, calls=%fused_computation.21 | convolution fusion | flops 3623878656 | bytes 11141120 | tf_op jit(solution)/shard_map/dot_general | solution.py:29
  204.8 0.0 all-gather.3.cloned.1.call-update
  204.8 73.4 %all-gather.3.cloned.1.call-done = f32[16384,128]{1,0:T(8,128)} async-done(((f32[1024,128]{1,0:T(8,128)}), f32[16384,128]{1,0:T(8,128)}) %all-gather.3.cloned.1.call-update) | async-done | bytes 8388624 | tf_op jit(solution)/shard_map/all_gather | solution.py:21
  278.2 3.8 %reduce_sum.20 = f32[1024,128]{1,0:T(8,128)S(1)} reduce(f32[16,1024,128]{2,1,0:T(8,128)} %bitcast.22, f32[]{:T(128)} %constant.58.clone.1), dimensions={0}, to_apply=%region_4.5 | reduce | flops 1966080 | bytes 8912900 | tf_op jit(solution)/shard_map/reduce_sum | solution.py:22
  282.0 11.7 %subtract_convert_fusion = (bf16[2304,1024]{1,0:T(8,128)(2,1)}, f32[2304,1024]{1,0:T(8,128)S(1)}) fusion(f32[2304,1024]{1,0:T(8,128)} %copy-done.1, f32[128,2304]{1,0:T(8,128)S(1)} %fusion.4, f32[1024,128]{1,0:T(8,128)S(1)} %reduce_sum.20), kind=kOutput, calls=%fused_computation | convolution fusion | flops 3628728320 | bytes 25296896 | tf_op jit(solution)/shard_map/dot_general | solution.py:31
  293.7 0.9 constant_dynamic-slice_fusion
  (2 shorter events, 0.1 us)
Async XLA Ops:
  7.2 1.1 copy-start
  7.2 7.0 %copy-start.3 = (f32[1024,128]{1,0:T(8,128)S(1)}, f32[1024,128]{1,0:T(8,128)}, u32[]{:S(2)}) copy-start(f32[1024,128]{1,0:T(8,128)} %param.5) | copy-start | bytes 1572868
  7.2 150.2 %all-reduce.2.cloned.1.call-start = ((), (), s32[]{:S(2)}) async-start(), calls=%async_computation | async-start | bytes 2359296 | tf_op jit(solution)/shard_map/psum | solution.py:27
  10.6 3.6 %copy-start.1 = (f32[2304,1024]{1,0:T(8,128)}, f32[2304,1024]{1,0:T(8,128)S(1)}, u32[]{:S(2)}) copy-start(f32[2304,1024]{1,0:T(8,128)S(1)} %fusion.9) | copy-start | bytes 28311556
  22.8 255.4 %all-gather.3.cloned.1.call-start = ((), (), s32[]{:S(2)}) async-start(), calls=%async_computation.1 | async-start | bytes 8912896 | tf_op jit(solution)/shard_map/all_gather | solution.py:21
  157.4 28.0 %copy-start.2 = (f32[2304,128]{1,0:T(8,128)S(1)}, f32[2304,128]{1,0:T(8,128)}, u32[]{:S(2)}) copy-start(f32[2304,128]{1,0:T(8,128)} %all-reduce.2.cloned.1.call-done) | copy-start | bytes 3538948
Sparse Core Ops, SparseCore 0:
  22.9 134.3 all-reduce.1
  204.9 73.2 all-gather.2
